TPU v7x, 256 devices: a whole 4x4x8 slice. The times are simulated.
256 devices in a mesh: row: 128 (over y, z, x), grp: 2 (over core).
Axes of the slice: x: 4, y: 4, z: 8, core: 2. Of those that a mesh axis runs over, the one named last changes fastest.
Arguments:
- features: float32 [1048576, 256], P(('row', 'grp')), may hold values from -6 to 6
- session: int32 [1048576], P(('row', 'grp')), may hold values from 0 to 8191, never falling along the last dimension, each value on 1 to 163840 neighbouring positions
- owner_map: int32 [256, 64], P(('row', 'grp')), may hold values from 0 to 127, as said below
Outputs:
- received: bfloat16 [32768, 64, 256], P(('row', 'grp'))
Inputs may be any that keep to these rules, and one draw needn't show every extreme that they name: session numbers never fall along the rows; each session covers 1 to 163840 consecutive rows. `owner_map`: no owner is named by more than 1 of the blocks of one group of 64.
All inputs are finite; a program needn't handle non-finite values.
Results may differ from a plain program's by a relative error of at most 0.001.
Values may be sent and summed in bfloat16 or wider, within the bound.
A program may use at most 128 MiB of HBM per device.

v0:
```python
import jax
import jax.numpy as jnp
from jax import lax
from jax.sharding import Mesh
from jax.sharding import PartitionSpec as P

ROW = ("row_0", "row_1", "row_2")
ROW_GRP = ("row_0", "row_1", "row_2", "grp")


def filled_with(array, identity):
    return jax.tree.map(
        lambda part, zero: jnp.zeros_like(part) + jnp.asarray(zero, part.dtype), array, identity
    )


def collected_together(array, axis):
    leaves = jax.tree.leaves(array)
    order = sorted(range(len(leaves)), key=lambda k: -leaves[k].size)
    width = (1, *leaves[order[0]].shape)[-1]
    lines = [
        jnp.pad(leaves[k].reshape(-1), (0, -leaves[k].size % width)).reshape(-1, width)
        for k in order
    ]
    both, at, found = (lax.all_gather(jnp.concatenate(lines), axis), 0, {})
    for k, line in zip(order, lines):
        section = both[:, at : at + len(line)].reshape(len(both), -1)
        found[k] = section[:, : leaves[k].size].reshape(-1, *leaves[k].shape)
        at += len(line)
    numbers = iter(range(len(leaves)))
    return jax.tree.map(lambda _: found[next(numbers)], array)


def carried_in(array, axes, combine, identity):
    before = start = filled_with(array, identity)
    so_far = array
    for axis in reversed(axes):
        size, here = (lax.axis_size(axis), lax.axis_index(axis))
        pieces = collected_together(so_far, axis)
        inside, so_far = (start, start)
        for k in range(size):
            passed = k < here
            so_far = combine(so_far, jax.tree.map(lambda part: part[k], pieces))
            inside = jax.tree.map(lambda new, old: jnp.where(passed, new, old), so_far, inside)
        before = combine(inside, before)
    return before


def local_sums(features, session, block_count):
    rows_dev, feature_width = features.shape
    block_rows = rows_dev // block_count
    grouped = features.reshape(block_count, block_rows, feature_width)
    grouped_ids = session.reshape(block_count, block_rows)
    position = jnp.arange(block_rows)
    same_mask = (
        (grouped_ids[:, :, None] == grouped_ids[:, None, :])
        & (position[None, None, :] <= position[None, :, None])
    ).astype(jnp.float32)
    inside = jnp.einsum("bij,bjf->bif", same_mask, grouped, precision=lax.Precision.HIGHEST)
    inside_count = jnp.sum(same_mask, axis=2)
    first_ids = grouped_ids[:, 0]
    row_index = jnp.arange(rows_dev)
    block_start = jnp.arange(block_count) * block_rows
    earlier_rows = (
        (session[None, :] == first_ids[:, None]) & (row_index[None, :] < block_start[:, None])
    ).astype(jnp.float32)
    carried = jnp.dot(earlier_rows, features, precision=lax.Precision.HIGHEST)
    carried_count = jnp.sum(earlier_rows, axis=1)
    joined = grouped_ids == first_ids[:, None]
    partial_rows = inside + jnp.where(joined[:, :, None], carried[:, None, :], 0.0)
    partial_count = inside_count + jnp.where(joined, carried_count[:, None], 0.0)
    return (partial_rows.reshape(rows_dev, feature_width), partial_count.reshape(rows_dev))


def chain_join(earlier, latter):
    early_meta, early_tail = earlier
    late_meta, late_tail = latter
    first_id = jnp.where(early_meta[0] < 0, late_meta[0], early_meta[0])
    last_id = jnp.where(late_meta[1] < 0, early_meta[1], late_meta[1])
    joined = (late_meta[0] < 0) | (late_meta[0] == late_meta[1]) & (early_meta[1] == late_meta[0])
    count_rows = late_meta[2] + jnp.where(joined, early_meta[2], 0.0)
    tail_sum = late_tail + jnp.where(joined, early_tail, 0.0)
    return (jnp.stack([first_id, last_id, count_rows]), tail_sum)


def body(features, session, owner_map):
    rows_dev, feature_width = features.shape
    owners = owner_map[0]
    block_count = owners.shape[0]
    block_rows = rows_dev // block_count
    row_count = lax.axis_size(ROW)
    slot_cap = max(1, 2 * block_count // row_count)
    partial_rows, partial_count = local_sums(features, session, block_count)
    session_float = session.astype(jnp.float32)
    tail_sum = partial_rows[-1]
    tail_count = partial_count[-1]
    own_meta = jnp.stack([session_float[0], session_float[-1], tail_count])
    identity = (jnp.array([-1.0, -1.0, 0.0], jnp.float32), jnp.zeros((feature_width,), jnp.float32))
    carry_meta, carry_tail = carried_in((own_meta, tail_sum), ROW_GRP, chain_join, identity)
    order = jnp.arange(block_count)
    rank = jnp.sum(
        ((owners[:, None] == owners[None, :]) & (order[None, :] < order[:, None])).astype(
            jnp.int32
        ),
        axis=1,
    )
    target = owners * slot_cap + rank
    slot_index = jnp.arange(row_count * slot_cap)
    hit = slot_index[:, None] == target[None, :]
    filled = jnp.any(hit, axis=1)
    source = jnp.sum(jnp.where(hit, order[None, :], 0), axis=1)
    joined = session_float == carry_meta[1]
    total = partial_rows + jnp.where(joined[:, None], carry_tail[None, :], 0.0)
    counted = partial_count + jnp.where(joined, carry_meta[2], 0.0)
    normalized = (total / jnp.sqrt(counted)[:, None]).astype(jnp.bfloat16)
    normalized = normalized.reshape(block_count, block_rows, feature_width)
    outgoing = jnp.where(filled[:, None, None], normalized[source], jnp.zeros((), jnp.bfloat16))
    return lax.all_to_all(outgoing, ROW, split_axis=0, concat_axis=0, tiled=True)


def solution(mesh):
    split = Mesh(
        mesh.devices.reshape(4, 8, 4, mesh.shape["grp"]), ("row_0", "row_1", "row_2", "grp")
    )
    return jax.shard_map(
        body,
        mesh=split,
        in_specs=(P(ROW_GRP, None), P(ROW_GRP), P(ROW_GRP, None)),
        out_specs=P(ROW_GRP, None, None),
        check_vma=False,
    )
```

profile of v0, /device:TPU:32, one launch (start us, length us, event | category | flops | bytes accessed | tf_op | source)
XLA Modules:
  0.0 279.7 jit_solution(9841545051146647536)
XLA Ops:
  0.0 0.9 convert_reduce_fusion.2
  0.9 0.7 fusion.27
  1.6 0.1 select_reduce_fusion
  1.7 0.1 fusion.9
  1.8 0.7 convert_element_type.22
  2.5 0.8 eq.221
  3.3 0.6 fusion.30
  3.9 0.1 slice_reduce_fusion
  4.0 0.1 iota_compare_fusion.1
  4.0 1.1 convert_reduce_fusion.1
  5.1 0.1 broadcast_in_dim.136
  5.2 0.1 broadcast_in_dim.137
  5.3 1.3 convert_reduce_fusion
  6.6 0.1 reduce_sum.45
  6.7 0.1 eq.225
  6.7 0.1 eq.230
  6.8 0.9 select_add_fusion.1
  7.7 0.6 slice.701
  8.3 4.1 %fusion.4 = f32[64,256]{1,0:T(8,128)S(1)} fusion(f32[4096,256]{1,0:T(8,128)} %param.4, s32[64]{0:T(128)S(1)} %iota_multiply_fusion, s32[4096]{0:T(1024)} %param.5, s32[64]{0:T(128)S(1)} %slice_reduce_fusion), kind=kOutput, calls=%fused_computation.12 | convolution fusion | flops 806092800 | bytes 4276736 | tf_op jit(solution)/shard_map/dot_general | solution.py:67
  12.4 0.0 copy-start.3
  12.4 3.1 %select_add_fusion = f32[64,64,256]{2,1,0:T(8,128)S(1)} fusion(f32[64,64,256]{2,1,0:T(8,128)S(1)} %bitcast.166, f32[64,256]{1,0:T(8,128)S(1)} %fusion.4, pred[64,64]{1,0:T(8,128)(4,1)S(1)} %get-tuple-element.85, s32[64,64]{1,0:T(8,128)S(1)} %eq.221, pred[64,64]{1,0:T(8,128)(4,1)S(1)} %get-tuple-element.84), kind=kOutput, calls=%fused_computation.2 | convolution fusion | flops 807927808 | bytes 8478720 | tf_op jit(solution)/shard_map/bij,bjf->bif/dot_general | solution.py:59
  15.5 0.0 copy-start
  15.5 2.0 copy-done
  17.6 1.9 select_maximum_fusion
  19.4 1.8 all-gather.4
  21.3 0.7 fusion.35
  30.1 1.2 broadcast_select_fusion.53
  31.4 0.6 fusion.39
  34.4 11.2 %all-gather.5 = f32[4,2,256]{2,1,0:T(2,128)S(1)} all-gather(f32[1,2,256]{2,1,0:T(2,128)S(1)} %maximum_bitcast_fusion.1), channel_id=3, replica_groups=mesh['row_0'=4,'row_1'=8,'row_2'=4,'grp'=2] {'row_2'}, dimensions={0}, use_global_device_ids=true | all-gather | bytes 10240 | tf_op jit(solution)/shard_map/all_gather | solution.py:25
  45.6 0.7 fusion.34
  64.2 1.3 broadcast_select_fusion.51
  65.4 0.6 fusion.38
  69.2 23.7 %all-gather.6 = f32[8,2,256]{2,1,0:T(2,128)S(1)} all-gather(f32[1,2,256]{2,1,0:T(2,128)S(1)} %maximum_bitcast_fusion.2), channel_id=4, replica_groups=mesh['row_0'=4,'row_1'=8,'row_2'=4,'grp'=2] {'row_1'}, dimensions={0}, use_global_device_ids=true | all-gather | bytes 18432 | tf_op jit(solution)/shard_map/all_gather | solution.py:25
  92.9 0.6 fusion.32
  93.5 0.7 fusion.31
  132.2 1.3 broadcast_select_fusion.47
  133.5 0.7 fusion.37
  136.8 11.3 %all-gather.7 = f32[4,2,256]{2,1,0:T(2,128)S(1)} all-gather(f32[1,2,256]{2,1,0:T(2,128)S(1)} %maximum_bitcast_fusion.3), channel_id=5, replica_groups=mesh['row_0'=4,'row_1'=8,'row_2'=4,'grp'=2] {'row_0'}, dimensions={0}, use_global_device_ids=true | all-gather | bytes 10240 | tf_op jit(solution)/shard_map/all_gather | solution.py:25
  148.1 0.7 fusion.33
  167.9 1.3 broadcast_select_fusion.39
  169.2 0.6 fusion.36
  172.3 0.1 broadcast_in_dim.141
  172.3 0.1 div.11
  172.4 3.6 %divide_convert_fusion = bf16[64,64,256]{2,1,0:T(8,128)(2,1)S(1)} fusion(f32[64,64,256]{2,1,0:T(8,128)} %copy-done, f32[64,64]{1,0:T(8,128)S(1)} %div.11, f32[256]{0:T(256)S(1)} %add_add_fusion, pred[64,64]{1,0:T(8,128)(4,1)S(1)} %broadcast_in_dim.141), kind=kLoop, calls=%fused_computation.1 | loop fusion | flops 4194304 | bytes 6312960 | tf_op jit(solution)/shard_map/convert_element_type | solution.py:115
  176.0 2.8 %gather_fusion = bf16[128,64,256]{2,1,0:T(8,128)(2,1)} fusion(bf16[64,64,256]{2,1,0:T(8,128)(2,1)S(1)} %divide_convert_fusion, s32[1024]{0:T(1024)S(1)} %pad_clamp_fusion), kind=kCustom, calls=%fused_computation | custom fusion | bytes 8389120 | tf_op jit(solution)/shard_map/gather | solution.py:117
  178.8 2.5 broadcast_select_fusion
  181.4 96.3 %all_to_all.5 = bf16[128,64,256]{2,1,0:T(8,128)(2,1)S(1)} all-to-all(bf16[128,64,256]{2,1,0:T(8,128)(2,1)S(1)} %broadcast_select_fusion), channel_id=1, replica_groups=mesh['row_0'=4,'row_1'=8,'row_2'=4,'grp'=2] {'row_0','row_1','row_2'}, dimensions={0} | all-to-all | bytes 8388608 | tf_op jit(solution)/shard_map/all_to_all | solution.py:118
  277.7 2.0 copy.21
  (30 shorter events, 0.2 us)
Async XLA Ops:
  6.8 5.6 %copy-start.1 = (f32[4096,256]{1,0:T(8,128)S(1)}, f32[4096,256]{1,0:T(8,128)}, u32[]{:S(2)}) copy-start(f32[4096,256]{1,0:T(8,128)} %param.4) | copy-start | bytes 12582916
  12.4 17.7 %copy-start.3 = (f32[3]{0:T(128)S(1)}, f32[3]{0:T(128)}, u32[]{:S(2)}) copy-start(f32[3]{0:T(128)} %constant.46.clone) | copy-start | bytes 40
  12.4 159.8 %copy-start.2 = (s32[4096]{0:T(1024)S(1)}, s32[4096]{0:T(1024)}, u32[]{:S(2)}) copy-start(s32[4096]{0:T(1024)} %param.5) | copy-start | bytes 49156
  15.5 2.0 copy-start
where the time goes:
time: 282 us; the launch traced here: 280 us
  blocking collectives  144 us (51%)
  between operations  93.7 us (33%)
  other arithmetic  19.1 us (7%)
  local copies, waits for them, and re-layouts  15.4 us (5%)
  matrix products  7.19 us (3%)
    all_to_all x1, blocking collectives, body(): lax.all_to_all(outgoing, ROW, split_axis=0, concat_axis=0, tiled=True)  96.3 us
    all_gather x4, blocking collectives, collected_together(): both, at, found = (lax.all_gather(jnp.concatenate(lines), axis), 0, {})  48 us

commit v1 on v0

v1 whole, which is shorter than its diff:
```python
import jax
import jax.numpy as jnp
from jax import lax
from jax.experimental import pallas as pl
from jax.experimental.pallas import tpu as pltpu
from jax.sharding import Mesh
from jax.sharding import PartitionSpec as P

ROW = ("row_0", "row_1", "row_2")
ROW_GRP = ("row_0", "row_1", "row_2", "grp")
MOST = 163840
TILE = 128
MESH = pl.DeviceIdType.MESH


def coords(d, sizes):
    out = []
    for n in reversed(sizes):
        out.append(lax.rem(d, n))
        d = lax.div(d, n)
    return tuple(reversed(out))


def prelude_kernel(
    sizes, reach, block_rows,
    src_ref, ids_ref, feat_hbm, out_ref,
    feat, idcol, cnt, norm, tail, got, load_sem, send_sem, recv_sem,
):
    total_devices = 1
    for n in sizes:
        total_devices *= n
    me = lax.axis_index(ROW_GRP)
    rows_dev, width = feat.shape
    tiles = rows_dev // TILE
    chunks = load_sem.shape[0]
    per = rows_dev // chunks

    def load(c):
        at = pl.ds(c * per, per)
        return pltpu.make_async_copy(feat_hbm.at[at], feat.at[at], load_sem.at[c])

    for c in range(chunks):
        load(c).start()

    barrier = pltpu.get_barrier_semaphore()

    @pl.loop(1, reach + 1)
    def _(k):
        peer = lax.rem(me + total_devices - k, total_devices)
        pl.semaphore_signal(barrier, 1, device_id=coords(peer, sizes), device_id_type=MESH)

    last = ids_ref[tiles - 1 : tiles, TILE - 1 : TILE]
    last_wide = jnp.broadcast_to(last, (TILE, TILE))

    sums = jnp.zeros((8, width), jnp.float32)
    count = jnp.zeros((8, TILE), jnp.float32)
    for c in range(chunks):
        load(c).wait()

        @pl.loop(c * (tiles // chunks), (c + 1) * (tiles // chunks), init_carry=(sums, count))
        def tail_step(t, carry):
            acc, num = carry
            wide = jnp.broadcast_to(ids_ref[pl.ds(t, 1), :], (TILE, TILE))
            col = wide.T
            at = pl.ds(pl.multiple_of(t * TILE, TILE), TILE)
            idcol[at, :] = col
            open_rows = col == last_wide
            both = jnp.concatenate([open_rows, open_rows], axis=1)
            rows = jnp.where(both, feat[at, :], 0.0)
            acc = acc + jnp.sum(rows.reshape(TILE // 8, 8, width), axis=0)
            num = num + jnp.sum(
                jnp.where(open_rows, 1.0, 0.0).reshape(TILE // 8, 8, TILE), axis=0
            )
            return acc, num

        sums, count = tail_step
    sums = jnp.sum(sums, axis=0, keepdims=True)
    count = jnp.sum(count, axis=0, keepdims=True)
    tail[0:1, :] = sums[:, :TILE]
    tail[1:2, :] = sums[:, TILE:]
    tail[2:3, :] = jnp.broadcast_to(last, (1, TILE))
    tail[3:4, :] = count

    pl.semaphore_wait(barrier, reach)

    @pl.loop(1, reach + 1)
    def _(k):
        peer = lax.rem(me + k, total_devices)
        pltpu.make_async_remote_copy(
            src_ref=tail,
            dst_ref=got.at[k - 1],
            send_sem=send_sem,
            recv_sem=recv_sem,
            device_id=coords(peer, sizes),
            device_id_type=MESH,
        ).start()

    above = lax.broadcasted_iota(jnp.int32, (TILE, TILE), 0)
    left = lax.broadcasted_iota(jnp.int32, (TILE, TILE), 1)
    causal = left <= above
    ones = jnp.ones((TILE, TILE), jnp.bfloat16)

    @pl.loop(
        0, tiles,
        init_carry=(
            jnp.full((1, TILE), -1.0, jnp.float32),
            jnp.zeros((1, width), jnp.float32),
            jnp.zeros((1, TILE), jnp.float32),
        ),
        unroll=2,
    )
    def _(t, carry):
        open_id, open_sum, open_count = carry
        at = pl.ds(pl.multiple_of(t * TILE, TILE), TILE)
        col = idcol[at, :]
        wide = jnp.broadcast_to(ids_ref[pl.ds(t, 1), :], (TILE, TILE))
        mask = jnp.where((col == wide) & causal, 1.0, 0.0).astype(jnp.bfloat16)
        rows = feat[at, :]
        high = rows.astype(jnp.bfloat16)
        rest = rows - high.astype(jnp.float32)
        mid = rest.astype(jnp.bfloat16)
        low = (rest - mid.astype(jnp.float32)).astype(jnp.bfloat16)
        inside = (
            jnp.dot(mask, high, preferred_element_type=jnp.float32)
            + jnp.dot(mask, mid, preferred_element_type=jnp.float32)
            + jnp.dot(mask, low, preferred_element_type=jnp.float32)
        )
        number = jnp.dot(mask, ones, preferred_element_type=jnp.float32)
        joined = col == jnp.broadcast_to(open_id, (TILE, TILE))
        both = jnp.concatenate([joined, joined], axis=1)
        inside = inside + jnp.where(both, jnp.broadcast_to(open_sum, (TILE, width)), 0.0)
        number = number + jnp.where(joined, jnp.broadcast_to(open_count, (TILE, TILE)), 0.0)
        feat[at, :] = inside
        cnt[at, :] = number
        return col[TILE - 1 :, :], inside[TILE - 1 :, :], number[TILE - 1 :, :]

    pltpu.make_async_copy(got, got, recv_sem).wait()
    arrived = got[...]
    open_id = arrived[0, 2:3, :]
    age = lax.broadcasted_iota(jnp.int32, arrived.shape, 0) + 1
    same = jnp.broadcast_to(arrived[:, 2:3, :], arrived.shape) == jnp.broadcast_to(
        open_id[None], arrived.shape
    )
    merged = jnp.sum(jnp.where(same & (age <= me), arrived, 0.0), axis=0)
    open_sum = jnp.concatenate([merged[0:1, :], merged[1:2, :]], axis=1)
    open_count = merged[3:4, :]

    @pl.loop(0, rows_dev // block_rows, unroll=2)
    def _(b):
        at = pl.ds(pl.multiple_of(b * block_rows, block_rows), block_rows)
        joined = idcol[at, :] == jnp.broadcast_to(open_id, (block_rows, TILE))
        number = cnt[at, :] + jnp.where(
            joined, jnp.broadcast_to(open_count, (block_rows, TILE)), 0.0
        )
        scale = 1.0 / jnp.sqrt(number)
        both = jnp.concatenate([joined, joined], axis=1)
        rows = feat[at, :] + jnp.where(
            both, jnp.broadcast_to(open_sum, (block_rows, width)), 0.0
        )
        norm[b] = (rows * jnp.concatenate([scale, scale], axis=1)).astype(jnp.bfloat16)

    @pl.loop(0, out_ref.shape[0], unroll=4)
    def _(slot):
        b = src_ref[slot]
        block = norm[jnp.maximum(b, 0)]
        out_ref[slot] = jnp.where(b >= 0, block, jnp.zeros_like(block))

    pltpu.make_async_copy(got, got, send_sem).wait()


def body(features, session, owner_map):
    rows_dev, width = features.shape
    owners = owner_map[0]
    block_count = owners.shape[0]
    block_rows = rows_dev // block_count
    row_count = lax.axis_size(ROW)
    sizes = tuple(lax.axis_size(name) for name in ROW_GRP)
    slot_cap = max(1, 2 * block_count // row_count)
    slots = row_count * slot_cap
    order = jnp.arange(block_count)
    rank = jnp.sum(
        ((owners[:, None] == owners[None, :]) & (order[None, :] < order[:, None])).astype(
            jnp.int32
        ),
        axis=1,
    )
    target = owners * slot_cap + rank
    hit = jnp.arange(slots)[:, None] == target[None, :]
    source = jnp.sum(jnp.where(hit, order[None, :] + 1, 0), axis=1).astype(jnp.int32) - 1
    reach = (MOST - 2) // rows_dev + 1
    ids = session.astype(jnp.float32).reshape(rows_dev // TILE, TILE)
    outgoing = pl.pallas_call(
        lambda *refs: prelude_kernel(sizes, reach, block_rows, *refs),
        out_shape=jax.ShapeDtypeStruct((slots, block_rows, width), jnp.bfloat16),
        in_specs=[
            pl.BlockSpec(memory_space=pltpu.SMEM),
            pl.BlockSpec(memory_space=pltpu.VMEM),
            pl.BlockSpec(memory_space=pl.ANY),
        ],
        out_specs=pl.BlockSpec(memory_space=pltpu.VMEM),
        scratch_shapes=[
            pltpu.VMEM((rows_dev, width), jnp.float32),
            pltpu.VMEM((rows_dev, TILE), jnp.float32),
            pltpu.VMEM((rows_dev, TILE), jnp.float32),
            pltpu.VMEM((block_count, block_rows, width), jnp.bfloat16),
            pltpu.VMEM((4, TILE), jnp.float32),
            pltpu.VMEM((reach, 4, TILE), jnp.float32),
            pltpu.SemaphoreType.DMA((4,)),
            pltpu.SemaphoreType.DMA,
            pltpu.SemaphoreType.DMA,
        ],
        compiler_params=pltpu.CompilerParams(collective_id=0, has_side_effects=True),
        name="prelude",
    )(source, ids, features)
    return lax.all_to_all(outgoing, ROW, split_axis=0, concat_axis=0, tiled=True)


def solution(mesh):
    split = Mesh(
        mesh.devices.reshape(4, 8, 4, mesh.shape["grp"]), ("row_0", "row_1", "row_2", "grp")
    )
    return jax.shard_map(
        body,
        mesh=split,
        in_specs=(P(ROW_GRP, None), P(ROW_GRP), P(ROW_GRP, None)),
        out_specs=P(ROW_GRP, None, None),
        check_vma=False,
    )
```

time: 282 us -> 136 us (0.48)
  between operations: 93.7 us -> 0.02 us
  blocking collectives: 144 us -> 107 us
  Pallas kernels: 0 us -> 23.1 us
  other arithmetic: 19.1 us -> 3.53 us
  local copies, waits for them, and re-layouts: 15.4 us -> 2.01 us
  matrix products: 7.19 us -> 0 us
    all_gather x4 -> x0, blocking collectives: 48 us -> none  [collected_together(): both, at, found = (lax.all_gather(jnp.concatenate(lines), axis), 0, {})]
    pallas_call x0 -> x1, Pallas kernels: none -> 23.1 us  [body(): pl.pallas_call(lambda *refs: prelude_kernel(sizes, reach, block_rows, *re...]
    all_to_all x1, blocking collectives: 96.3 us -> 107 us  [body(): lax.all_to_all(outgoing, ROW, split_axis=0, concat_axis=0, tiled=True)]
    select_n x8 -> x0, other arithmetic: 7.75 us -> none  [the longest x4 5.16 us: carried_in(): jnp.where(passed, new, old)]
    dot_general x2 -> x0, matrix products: 7.19 us -> none  [the longest x1 4.08 us: local_sums(): carried = jnp.dot(earlier_rows, features, precision=lax.Precision.HIGHEST)]
    slice x17 -> x0, local copies, waits for them, and re-layouts: 7.16 us -> none  [the longest x4 2.7 us: chain_join(): last_id = jnp.where(late_meta[1] < 0, early_meta[1], late_meta[1])]
    convert_element_type x2 -> x0, other arithmetic: 4.32 us -> none  [the longest x1 3.59 us: body(): normalized = (total / jnp.sqrt(counted)[:, None]).astype(jnp.bfloat16)]
    gather x1 -> x0, local copies, waits for them, and re-layouts: 2.83 us -> none  [body(): normalized[source]]
where the time goes in v1:
time: 136 us
  blocking collectives  107 us (79%)
  Pallas kernels  23.1 us (17%)
  other arithmetic  3.53 us (3%)
  local copies, waits for them, and re-layouts  2.01 us (1%)
    all_to_all x1, blocking collectives, body(): lax.all_to_all(outgoing, ROW, split_axis=0, concat_axis=0, tiled=True)  107 us
    pallas_call x1, Pallas kernels, body(): pl.pallas_call(lambda *refs: prelude_kernel(sizes, reach, block_rows, *re...  23.1 us

profile of v1, /device:TPU:32, one launch (start us, length us, event | category | flops | bytes accessed | tf_op | source)
XLA Modules:
  0.0 136.1 jit_solution(14294477747002663696)
XLA Ops:
  0.0 0.9 convert_reduce_fusion
  0.9 0.7 fusion.1
  1.6 0.1 select_reduce_fusion
  1.7 0.5 broadcast_add_fusion.refs_0_
  2.2 1.3 convert_bitcast_fusion.refs_1_
  3.5 23.1 %prelude.1 = bf16[128,64,256]{2,1,0:T(8,128)(2,1)} custom-call(s32[128]{0:T(128)} %broadcast_add_fusion.refs_0_, f32[32,128]{1,0:T(8,128)} %convert_bitcast_fusion.refs_1_, f32[4096,256]{1,0:T(8,128)} %refs_2_.1), custom_call_target="tpu_custom_call" | custom-call | tf_op jit(solution)/shard_map/prelude/pallas_call | solution.py:192
  26.7 107.4 %all_to_all.5 = bf16[128,64,256]{2,1,0:T(8,128)(2,1)S(1)} all-to-all(bf16[128,64,256]{2,1,0:T(8,128)(2,1)} %prelude.1), channel_id=1, replica_groups=mesh['row_0'=4,'row_1'=8,'row_2'=4,'grp'=2] {'row_0','row_1','row_2'}, dimensions={0} | all-to-all | bytes 8388608 | tf_op jit(solution)/shard_map/all_to_all | solution.py:215
  134.0 2.0 %copy.5 = bf16[128,64,256]{2,1,0:T(8,128)(2,1)} copy(bf16[128,64,256]{2,1,0:T(8,128)(2,1)S(1)} %all_to_all.5) | data formatting | bytes 8388608
  (1 shorter events, 0.0 us)

commit v2 on v1

v2 whole, which is shorter than its diff:
```python
import jax
import jax.numpy as jnp
from jax import lax
from jax.experimental import pallas as pl
from jax.experimental.pallas import tpu as pltpu
from jax.sharding import Mesh
from jax.sharding import PartitionSpec as P

ROW = ("row_0", "row_1", "row_2")
ROW_GRP = ("row_0", "row_1", "row_2", "grp")
MOST = 163840
TILE = 128
MESH = pl.DeviceIdType.MESH


def coords(d, sizes):
    out = []
    for n in reversed(sizes):
        out.append(lax.rem(d, n))
        d = lax.div(d, n)
    return tuple(reversed(out))


def prelude_kernel(
    sizes, reach, block_rows, slot_cap,
    owners_hbm, ids_hbm, feat_hbm, out_ref,
    owners_ref, ids_ref, feat, sums, cnt, norm, ends, joins, table, slot_of, tail, got,
    load_sem, table_sem, send_sem, recv_sem,
):
    total_devices = 1
    for n in sizes:
        total_devices *= n
    me = lax.axis_index(ROW_GRP)
    rows_dev, width = feat.shape
    tiles = rows_dev // TILE
    blocks = rows_dev // block_rows
    slots = out_ref.shape[0]
    loads = [
        pltpu.make_async_copy(src, dst, load_sem.at[n])
        for n, (src, dst) in enumerate(
            ((ids_hbm, ids_ref), (owners_hbm, owners_ref), (feat_hbm, feat))
        )
    ]
    for load in loads:
        load.start()

    barrier = pltpu.get_barrier_semaphore()

    @pl.loop(1, reach + 1)
    def _(k):
        peer = lax.rem(me + total_devices - k, total_devices)
        pl.semaphore_signal(barrier, 1, device_id=coords(peer, sizes), device_id_type=MESH)

    loads[0].wait()
    ids = ids_ref[...]
    last = jnp.broadcast_to(ids[tiles - 1 :, TILE - 1 :], (1, TILE))
    in_last = jnp.where(ids == jnp.broadcast_to(last, ids.shape), 1.0, 0.0)
    count = jnp.sum(jnp.sum(in_last, axis=0, keepdims=True), axis=1, keepdims=True)
    first = jnp.broadcast_to(rows_dev - count.astype(jnp.int32), (8, width))
    step = 64
    loads[2].wait()
    sub = lax.broadcasted_iota(jnp.int32, (step, width), 0)

    @pl.loop(0, rows_dev // step, init_carry=jnp.zeros((step, width), jnp.float32), unroll=4)
    def open_rows(t, acc):
        at = pl.ds(pl.multiple_of(t * step, step), step)
        inside = sub + t * step >= jnp.broadcast_to(first[0:1], (step, width))
        return acc + jnp.where(inside, feat[at, :], 0.0)

    total = jnp.sum(open_rows, axis=0, keepdims=True)
    tail[0:1, :] = total[:, :TILE]
    tail[1:2, :] = total[:, TILE:]
    tail[2:3, :] = last.astype(jnp.float32)
    tail[3:4, :] = jnp.broadcast_to(count, (1, TILE))

    lane = lax.broadcasted_iota(jnp.int32, ids.shape, 1)
    after = pltpu.roll(ids, TILE - 1, 1)
    end = jnp.where((after != ids) | (lane == TILE - 1), lane, TILE)
    hop = 1
    while hop < TILE:
        ahead = jnp.where(lane + hop < TILE, pltpu.roll(end, TILE - hop, 1), TILE)
        end = jnp.minimum(end, ahead)
        hop *= 2
    ends[...] = end
    before = jnp.concatenate([jnp.full((1, TILE), -1, jnp.int32), ids[:-1]], axis=0)
    before = jnp.broadcast_to(before[:, TILE - 1 :], ids.shape)
    goes_on = jnp.sum(jnp.where(ids == before, 1.0, 0.0), axis=1, keepdims=True)
    joins[...] = jnp.broadcast_to(goes_on.astype(jnp.int32), ids.shape)

    pl.semaphore_wait(barrier, reach)

    @pl.loop(1, reach + 1)
    def _(k):
        peer = lax.rem(me + k, total_devices)
        pltpu.make_async_remote_copy(
            src_ref=tail,
            dst_ref=got.at[k - 1],
            send_sem=send_sem,
            recv_sem=recv_sem,
            device_id=coords(peer, sizes),
            device_id_type=MESH,
        ).start()

    loads[1].wait()
    owners = owners_ref[...]
    across = jnp.broadcast_to(owners, (blocks, blocks))
    down = jnp.broadcast_to(across.T[:, 0:1], (blocks, blocks))
    earlier = lax.broadcasted_iota(jnp.int32, (blocks, blocks), 1) < (
        lax.broadcasted_iota(jnp.int32, (blocks, blocks), 0)
    )
    rank = jnp.sum(jnp.where((across == down) & earlier, 1.0, 0.0), axis=1, keepdims=True)
    target = down[:, 0:1] * slot_cap + rank.astype(jnp.int32)
    hit = jnp.broadcast_to(target, (blocks, slots)) == (
        lax.broadcasted_iota(jnp.int32, (blocks, slots), 1)
    )
    order = lax.broadcasted_iota(jnp.int32, (blocks, slots), 0) + 1
    table[...] = jnp.sum(jnp.where(hit, order, 0), axis=0, keepdims=True)
    to_scalars = pltpu.make_async_copy(table, slot_of, table_sem)
    to_scalars.start()

    row = lax.broadcasted_iota(jnp.int32, (TILE, TILE), 0)
    col = lax.broadcasted_iota(jnp.int32, (TILE, TILE), 1)
    causal = col <= row
    ones = jnp.ones((TILE, TILE), jnp.bfloat16)

    @pl.loop(
        0, tiles,
        init_carry=(jnp.zeros((1, width), jnp.float32), jnp.zeros((1, TILE), jnp.float32)),
        unroll=4,
    )
    def _(t, carry):
        open_sum, open_count = carry
        at = pl.ds(pl.multiple_of(t * TILE, TILE), TILE)
        alive = row <= jnp.broadcast_to(ends[pl.ds(t, 1), :], (TILE, TILE))
        mask = jnp.where(alive & causal, 1.0, 0.0).astype(jnp.bfloat16)
        rows = feat[at, :]
        high = rows.astype(jnp.bfloat16)
        rest = rows - high.astype(jnp.float32)
        mid = rest.astype(jnp.bfloat16)
        low = (rest - mid.astype(jnp.float32)).astype(jnp.bfloat16)
        inside = (
            jnp.dot(mask, high, preferred_element_type=jnp.float32)
            + jnp.dot(mask, mid, preferred_element_type=jnp.float32)
            + jnp.dot(mask, low, preferred_element_type=jnp.float32)
        )
        number = jnp.dot(mask, ones, preferred_element_type=jnp.float32)
        joined = row < jnp.broadcast_to(joins[pl.ds(t, 1), :], (TILE, TILE))
        both = jnp.concatenate([joined, joined], axis=1)
        inside = inside + jnp.where(both, jnp.broadcast_to(open_sum, (TILE, width)), 0.0)
        number = number + jnp.where(joined, jnp.broadcast_to(open_count, (TILE, TILE)), 0.0)
        sums[at, :] = inside
        cnt[at, :] = number
        return inside[TILE - 1 :, :], number[TILE - 1 :, :]

    pltpu.make_async_copy(got, got, recv_sem).wait()
    arrived = got[...]
    open_id = arrived[0, 2:3, :]
    age = lax.broadcasted_iota(jnp.int32, arrived.shape, 0) + 1
    same = jnp.broadcast_to(arrived[:, 2:3, :], arrived.shape) == jnp.broadcast_to(
        open_id[None], arrived.shape
    )
    merged = jnp.sum(jnp.where(same & (age <= me), arrived, 0.0), axis=0)
    open_sum = jnp.concatenate([merged[0:1, :], merged[1:2, :]], axis=1)
    open_count = merged[3:4, :]
    in_open = jnp.where(
        ids.astype(jnp.float32) == jnp.broadcast_to(open_id, ids.shape), 1.0, 0.0
    )
    reached = jnp.sum(jnp.sum(in_open, axis=0, keepdims=True), axis=1, keepdims=True)
    reached = jnp.broadcast_to(reached.astype(jnp.int32), (1, TILE))
    sub = lax.broadcasted_iota(jnp.int32, (block_rows, TILE), 0)

    @pl.loop(0, blocks, unroll=4)
    def _(b):
        at = pl.ds(pl.multiple_of(b * block_rows, block_rows), block_rows)
        joined = sub + b * block_rows < jnp.broadcast_to(reached, (block_rows, TILE))
        number = cnt[at, :] + jnp.where(
            joined, jnp.broadcast_to(open_count, (block_rows, TILE)), 0.0
        )
        scale = 1.0 / jnp.sqrt(number)
        both = jnp.concatenate([joined, joined], axis=1)
        rows = sums[at, :] + jnp.where(
            both, jnp.broadcast_to(open_sum, (block_rows, width)), 0.0
        )
        norm[b] = (rows * jnp.concatenate([scale, scale], axis=1)).astype(jnp.bfloat16)

    to_scalars.wait()

    @pl.loop(0, slots, unroll=8)
    def _(slot):
        b = slot_of[0, slot]
        block = norm[jnp.maximum(b, 1) - 1]
        out_ref[slot] = jnp.where(b > 0, block, jnp.zeros_like(block))

    pltpu.make_async_copy(got, got, send_sem).wait()


def body(features, session, owner_map):
    rows_dev, width = features.shape
    blocks = owner_map.shape[1]
    block_rows = rows_dev // blocks
    row_count = lax.axis_size(ROW)
    sizes = tuple(lax.axis_size(name) for name in ROW_GRP)
    slot_cap = max(1, 2 * blocks // row_count)
    slots = row_count * slot_cap
    tiles = rows_dev // TILE
    reach = (MOST - 2) // rows_dev + 1
    outgoing = pl.pallas_call(
        lambda *refs: prelude_kernel(sizes, reach, block_rows, slot_cap, *refs),
        out_shape=jax.ShapeDtypeStruct((slots, block_rows, width), jnp.bfloat16),
        in_specs=[pl.BlockSpec(memory_space=pltpu.HBM)] * 3,
        out_specs=pl.BlockSpec(memory_space=pltpu.VMEM),
        scratch_shapes=[
            pltpu.VMEM(owner_map.shape, jnp.int32),
            pltpu.VMEM((tiles, TILE), jnp.int32),
            pltpu.VMEM((rows_dev, width), jnp.float32),
            pltpu.VMEM((rows_dev, width), jnp.float32),
            pltpu.VMEM((rows_dev, TILE), jnp.float32),
            pltpu.VMEM((blocks, block_rows, width), jnp.bfloat16),
            pltpu.VMEM((tiles, TILE), jnp.int32),
            pltpu.VMEM((tiles, TILE), jnp.int32),
            pltpu.VMEM((1, slots), jnp.int32),
            pltpu.SMEM((1, slots), jnp.int32),
            pltpu.VMEM((4, TILE), jnp.float32),
            pltpu.VMEM((reach, 4, TILE), jnp.float32),
            pltpu.SemaphoreType.DMA((3,)),
            pltpu.SemaphoreType.DMA,
            pltpu.SemaphoreType.DMA,
            pltpu.SemaphoreType.DMA,
        ],
        compiler_params=pltpu.CompilerParams(
            collective_id=0, has_side_effects=True, vmem_limit_bytes=24 << 20
        ),
        name="prelude",
    )(owner_map, session.reshape(tiles, TILE), features)
    return lax.all_to_all(outgoing, ROW, split_axis=0, concat_axis=0, tiled=True)


def solution(mesh):
    split = Mesh(
        mesh.devices.reshape(4, 8, 4, mesh.shape["grp"]), ("row_0", "row_1", "row_2", "grp")
    )
    return jax.shard_map(
        body,
        mesh=split,
        in_specs=(P(ROW_GRP, None), P(ROW_GRP), P(ROW_GRP, None)),
        out_specs=P(ROW_GRP, None, None),
        check_vma=False,
    )
```

time: 136 us -> 134 us (0.985)
  Pallas kernels: 23.1 us -> 18.9 us
  local copies, waits for them, and re-layouts: 2.01 us -> 5.57 us
  other arithmetic: 3.53 us -> 0 us
  blocking collectives: 107 us -> 109 us
    pallas_call x1, Pallas kernels: 23.1 us -> 18.9 us  [body(): pl.pallas_call(lambda *refs: prelude_kernel(sizes, reach, block_rows, slo...]
    unnamed x1 -> x7, local copies, waits for them, and re-layouts: 2.01 us -> 5.57 us
    all_to_all x1, blocking collectives: 107 us -> 109 us  [body(): lax.all_to_all(outgoing, ROW, split_axis=0, concat_axis=0, tiled=True)]
where the time goes in v2:
time: 134 us; the launch traced here: 133 us
  blocking collectives  109 us (81%)
  Pallas kernels  18.9 us (14%)
  local copies, waits for them, and re-layouts  5.57 us (4%)
    all_to_all x1, blocking collectives, body(): lax.all_to_all(outgoing, ROW, split_axis=0, concat_axis=0, tiled=True)  109 us
    pallas_call x1, Pallas kernels, body(): pl.pallas_call(lambda *refs: prelude_kernel(sizes, reach, block_rows, slo...  18.9 us
    unnamed x7, local copies, waits for them, and re-layouts  5.57 us

profile of v2, /device:TPU:32, one launch (start us, length us, event | category | flops | bytes accessed | tf_op | source)
XLA Modules:
  0.0 133.3 jit_solution(15020178059859658627)
XLA Ops:
  0.0 0.0 copy-start
  0.0 2.2 %copy-done = f32[4096,256]{1,0:T(8,128)S(1)} copy-done((f32[4096,256]{1,0:T(8,128)S(1)}, f32[4096,256]{1,0:T(8,128)}, u32[]{:S(2)}) %copy-start) | copy-done | bytes 4194328
  2.2 0.0 copy-start.1
  2.2 0.7 copy-done.1
  2.9 0.0 copy-start.2
  2.9 0.7 copy-done.2
  3.6 18.9 %prelude.1 = bf16[128,64,256]{2,1,0:T(8,128)(2,1)S(1)} custom-call(s32[1,64]{1,0:T(1,128)S(1)} %copy-done.2, s32[32,128]{1,0:T(8,128)S(1)} %bitcast.1, f32[4096,256]{1,0:T(8,128)S(1)} %copy-done), custom_call_target="tpu_custom_call" | custom-call | tf_op jit(solution)/shard_map/prelude/pallas_call | solution.py:207
  22.5 108.8 %all_to_all.5 = bf16[128,64,256]{2,1,0:T(8,128)(2,1)S(1)} all-to-all(bf16[128,64,256]{2,1,0:T(8,128)(2,1)S(1)} %prelude.1), channel_id=1, replica_groups=mesh['row_0'=4,'row_1'=8,'row_2'=4,'grp'=2] {'row_0','row_1','row_2'}, dimensions={0} | all-to-all | bytes 8388608 | tf_op jit(solution)/shard_map/all_to_all | solution.py:235
  131.3 2.0 %copy.5 = bf16[128,64,256]{2,1,0:T(8,128)(2,1)} copy(bf16[128,64,256]{2,1,0:T(8,128)(2,1)S(1)} %all_to_all.5) | data formatting | bytes 8388608
Async XLA Ops:
  0.0 2.2 %copy-start = (f32[4096,256]{1,0:T(8,128)S(1)}, f32[4096,256]{1,0:T(8,128)}, u32[]{:S(2)}) copy-start(f32[4096,256]{1,0:T(8,128)} %refs_2_.1) | copy-start | bytes 12582916
  2.2 0.7 copy-start.1
  2.9 0.7 copy-start.2

commit v3 on v2

--- a/solution.py
+++ b/solution.py
@@ -10,6 +10,7 @@
 ROW_GRP = ("row_0", "row_1", "row_2", "grp")
 MOST = 163840
 TILE = 128
+ROOMS = (12, 13, 14, 15, 16)
 MESH = pl.DeviceIdType.MESH
 
 
@@ -21,20 +22,30 @@
     return tuple(reversed(out))
 
 
+def place():
+    return tuple(lax.axis_index(name) for name in ROW_GRP)
+
+
+def plane_order(y, x, nx):
+    return lax.rem(x + y, nx) * nx + y
+
+
 def prelude_kernel(
     sizes, reach, block_rows, slot_cap,
-    owners_hbm, ids_hbm, feat_hbm, out_ref,
-    owners_ref, ids_ref, feat, sums, cnt, norm, ends, joins, table, slot_of, tail, got,
-    load_sem, table_sem, send_sem, recv_sem,
+    owners_hbm, ids_hbm, feat_hbm,
+    norm, unpack_out, pack_out, most_out,
+    owners_ref, ids_ref, feat, sums, cnt, ends, joins, tail, got, mine, got_line, top, got_plane,
+    load_sem, send_sem, recv_sem, line_send, line_recv, plane_send, plane_recv,
 ):
-    total_devices = 1
-    for n in sizes:
-        total_devices *= n
+    ny, nz, nx, ng = sizes
+    devices = ny * nz * nx * ng
     me = lax.axis_index(ROW_GRP)
+    y, z, x, g = place()
     rows_dev, width = feat.shape
     tiles = rows_dev // TILE
     blocks = rows_dev // block_rows
-    slots = out_ref.shape[0]
+    line = nz * ng
+    plane = ny * nx
     loads = [
         pltpu.make_async_copy(src, dst, load_sem.at[n])
         for n, (src, dst) in enumerate(
@@ -44,12 +55,23 @@
     for load in loads:
         load.start()
 
+    def line_peer(j):
+        return (y, lax.rem(z + j // ng, nz), x, lax.rem(g + j % ng, ng))
+
+    def plane_peer(j):
+        return (lax.rem(y + j // nx, ny), z, lax.rem(x + j % nx, nx), g)
+
     barrier = pltpu.get_barrier_semaphore()
 
     @pl.loop(1, reach + 1)
     def _(k):
-        peer = lax.rem(me + total_devices - k, total_devices)
+        peer = lax.rem(me + devices - k, devices)
         pl.semaphore_signal(barrier, 1, device_id=coords(peer, sizes), device_id_type=MESH)
+
+    for j in range(1, line):
+        pl.semaphore_signal(barrier, 1, device_id=line_peer(j), device_id_type=MESH)
+    for j in range(1, plane):
+        pl.semaphore_signal(barrier, 1, device_id=plane_peer(j), device_id_type=MESH)
 
     loads[0].wait()
     ids = ids_ref[...]
@@ -58,8 +80,8 @@
     count = jnp.sum(jnp.sum(in_last, axis=0, keepdims=True), axis=1, keepdims=True)
     first = jnp.broadcast_to(rows_dev - count.astype(jnp.int32), (8, width))
     step = 64
+    sub = lax.broadcasted_iota(jnp.int32, (step, width), 0)
     loads[2].wait()
-    sub = lax.broadcasted_iota(jnp.int32, (step, width), 0)
 
     @pl.loop(0, rows_dev // step, init_carry=jnp.zeros((step, width), jnp.float32), unroll=4)
     def open_rows(t, acc):
@@ -73,50 +95,77 @@
     tail[2:3, :] = last.astype(jnp.float32)
     tail[3:4, :] = jnp.broadcast_to(count, (1, TILE))
 
+    loads[1].wait()
+    slots = ny * nz * nx * slot_cap
+    owners = owners_ref[...]
+    across = jnp.broadcast_to(owners, (blocks, blocks))
+    down = jnp.broadcast_to(across.T[:, 0:1], (blocks, blocks))
+    earlier = lax.broadcasted_iota(jnp.int32, (blocks, blocks), 1) < (
+        lax.broadcasted_iota(jnp.int32, (blocks, blocks), 0)
+    )
+    rank = jnp.sum(jnp.where((across == down) & earlier, 1.0, 0.0), axis=1, keepdims=True)
+    target = down[:, 0:1] * slot_cap + rank.astype(jnp.int32)
+    hit = jnp.broadcast_to(target, (blocks, slots)) == (
+        lax.broadcasted_iota(jnp.int32, (blocks, slots), 1)
+    )
+    used = jnp.sum(jnp.where(hit, 1.0, 0.0), axis=0, keepdims=True)
+    o_from = lax.broadcasted_iota(jnp.int32, (slots, slots), 0)
+    o_to = lax.broadcasted_iota(jnp.int32, (slots, slots), 1)
+
+    def plane_of(o):
+        return lax.rem(lax.div(o, nx), nz)
+
+    def order_of(o):
+        return plane_order(lax.div(o, nx * nz), lax.rem(o, nx), nx)
+
+    ahead = (plane_of(o_from) == plane_of(o_to)) & (order_of(o_from) < order_of(o_to))
+    before = jnp.dot(
+        jnp.broadcast_to(used, (8, slots)).astype(jnp.bfloat16),
+        jnp.where(ahead, 1.0, 0.0).astype(jnp.bfloat16),
+        preferred_element_type=jnp.float32,
+    )[0:1]
+    spot = jnp.where(used > 0.0, before + 1.0, 0.0)
+    mine[...] = spot.astype(jnp.int32)
+    key = plane_of(o_to[0:1]).astype(jnp.float32) * plane + before
+    block_key = jnp.sum(
+        jnp.where(hit, jnp.broadcast_to(key, (blocks, slots)), 0.0), axis=1, keepdims=True
+    )
+    entry = lax.broadcasted_iota(jnp.int32, (blocks, slots), 1).astype(jnp.float32)
+    order = lax.broadcasted_iota(jnp.int32, (blocks, slots), 0)
+    pack_out[...] = jnp.sum(
+        jnp.where(jnp.broadcast_to(block_key, (blocks, slots)) == entry, order, 0),
+        axis=0, keepdims=True,
+    )
+
     lane = lax.broadcasted_iota(jnp.int32, ids.shape, 1)
     after = pltpu.roll(ids, TILE - 1, 1)
     end = jnp.where((after != ids) | (lane == TILE - 1), lane, TILE)
     hop = 1
     while hop < TILE:
-        ahead = jnp.where(lane + hop < TILE, pltpu.roll(end, TILE - hop, 1), TILE)
-        end = jnp.minimum(end, ahead)
+        nxt = jnp.where(lane + hop < TILE, pltpu.roll(end, TILE - hop, 1), TILE)
+        end = jnp.minimum(end, nxt)
         hop *= 2
     ends[...] = end
-    before = jnp.concatenate([jnp.full((1, TILE), -1, jnp.int32), ids[:-1]], axis=0)
-    before = jnp.broadcast_to(before[:, TILE - 1 :], ids.shape)
-    goes_on = jnp.sum(jnp.where(ids == before, 1.0, 0.0), axis=1, keepdims=True)
+    prior = jnp.concatenate([jnp.full((1, TILE), -1, jnp.int32), ids[:-1]], axis=0)
+    prior = jnp.broadcast_to(prior[:, TILE - 1 :], ids.shape)
+    goes_on = jnp.sum(jnp.where(ids == prior, 1.0, 0.0), axis=1, keepdims=True)
     joins[...] = jnp.broadcast_to(goes_on.astype(jnp.int32), ids.shape)
 
-    pl.semaphore_wait(barrier, reach)
+    pl.semaphore_wait(barrier, reach + line - 1 + plane - 1)
 
     @pl.loop(1, reach + 1)
     def _(k):
-        peer = lax.rem(me + k, total_devices)
+        peer = lax.rem(me + k, devices)
         pltpu.make_async_remote_copy(
-            src_ref=tail,
-            dst_ref=got.at[k - 1],
-            send_sem=send_sem,
-            recv_sem=recv_sem,
-            device_id=coords(peer, sizes),
-            device_id_type=MESH,
+            src_ref=tail, dst_ref=got.at[k - 1], send_sem=send_sem, recv_sem=recv_sem,
+            device_id=coords(peer, sizes), device_id_type=MESH,
         ).start()
 
-    loads[1].wait()
-    owners = owners_ref[...]
-    across = jnp.broadcast_to(owners, (blocks, blocks))
-    down = jnp.broadcast_to(across.T[:, 0:1], (blocks, blocks))
-    earlier = lax.broadcasted_iota(jnp.int32, (blocks, blocks), 1) < (
-        lax.broadcasted_iota(jnp.int32, (blocks, blocks), 0)
-    )
-    rank = jnp.sum(jnp.where((across == down) & earlier, 1.0, 0.0), axis=1, keepdims=True)
-    target = down[:, 0:1] * slot_cap + rank.astype(jnp.int32)
-    hit = jnp.broadcast_to(target, (blocks, slots)) == (
-        lax.broadcasted_iota(jnp.int32, (blocks, slots), 1)
-    )
-    order = lax.broadcasted_iota(jnp.int32, (blocks, slots), 0) + 1
-    table[...] = jnp.sum(jnp.where(hit, order, 0), axis=0, keepdims=True)
-    to_scalars = pltpu.make_async_copy(table, slot_of, table_sem)
-    to_scalars.start()
+    for j in range(1, line):
+        pltpu.make_async_remote_copy(
+            src_ref=mine, dst_ref=got_line.at[j - 1], send_sem=line_send, recv_sem=line_recv,
+            device_id=line_peer(j), device_id_type=MESH,
+        ).start()
 
     row = lax.broadcasted_iota(jnp.int32, (TILE, TILE), 0)
     col = lax.broadcasted_iota(jnp.int32, (TILE, TILE), 1)
@@ -152,7 +201,25 @@
         cnt[at, :] = number
         return inside[TILE - 1 :, :], number[TILE - 1 :, :]
 
+    pltpu.make_async_copy(got_line, got_line, line_recv).wait()
+    spots = mine[...]
+    unpack_out[0:1, :] = spots
+    largest = spots
+    for j in range(1, line):
+        spots = got_line[j - 1]
+        largest = jnp.maximum(largest, spots)
+        if j % ng == 0:
+            unpack_out[j // ng : j // ng + 1, :] = spots
+    top[...] = largest
+
     pltpu.make_async_copy(got, got, recv_sem).wait()
+
+    for j in range(1, plane):
+        pltpu.make_async_remote_copy(
+            src_ref=top, dst_ref=got_plane.at[j - 1], send_sem=plane_send,
+            recv_sem=plane_recv, device_id=plane_peer(j), device_id_type=MESH,
+        ).start()
+
     arrived = got[...]
     open_id = arrived[0, 2:3, :]
     age = lax.broadcasted_iota(jnp.int32, arrived.shape, 0) + 1
@@ -183,56 +250,217 @@
         )
         norm[b] = (rows * jnp.concatenate([scale, scale], axis=1)).astype(jnp.bfloat16)
 
-    to_scalars.wait()
-
-    @pl.loop(0, slots, unroll=8)
-    def _(slot):
-        b = slot_of[0, slot]
-        block = norm[jnp.maximum(b, 1) - 1]
-        out_ref[slot] = jnp.where(b > 0, block, jnp.zeros_like(block))
-
+    pltpu.make_async_copy(got_plane, got_plane, plane_recv).wait()
+    for j in range(1, plane):
+        largest = jnp.maximum(largest, got_plane[j - 1])
+    most = jnp.max(largest.astype(jnp.float32), axis=1, keepdims=True).astype(jnp.int32)
+    most_out[...] = jnp.broadcast_to(most, most_out.shape)
     pltpu.make_async_copy(got, got, send_sem).wait()
+    pltpu.make_async_copy(got_line, got_line, line_send).wait()
+    pltpu.make_async_copy(got_plane, got_plane, plane_send).wait()
+
+
+def arrivals(sizes, room):
+    ny, nz, nx, ng = sizes
+    steps = []
+    for d in range(1, nz // 2):
+        steps += [(d, 0, room), (nz - d, 0, room)]
+    cuts = list(range(0, room, nx))[:ny] + [room]
+    return steps, [(nz // 2, a, b) for a, b in zip(cuts[:-1], cuts[1:])]
+
+
+def exchange_kernel(
+    sizes, room,
+    pack, unpack, norm, out,
+    send, stage, z_send, z_recv, p_send, p_recv, *recv,
+):
+    ny, nz, nx, ng = sizes
+    plane = ny * nx
+    y, z, x, g = place()
+    steps, parts = arrivals(sizes, room)
+    far = nz // 2
+    barrier = pltpu.get_barrier_semaphore()
+
+    def z_peer(d):
+        return (y, lax.rem(z + d, nz), x, g)
+
+    for d in range(1, nz):
+        pl.semaphore_signal(barrier, 1, device_id=z_peer(d), device_id_type=MESH)
+    for j in range(1, plane):
+        pl.semaphore_signal(
+            barrier, 1, device_id_type=MESH,
+            device_id=(lax.rem(y + j // nx, ny), z, lax.rem(x + j % nx, nx), g),
+        )
+
+    for d in [d for d, _, _ in steps] + [far]:
+        first = lax.rem(z + d, nz) * plane
+
+        @pl.loop(0, room)
+        def _(k):
+            send[d - 1, k] = norm[pack[0, first + k]]
+
+    pl.semaphore_wait(barrier, nz - 1 + plane - 1)
+
+    for n, (d, a, b) in enumerate(steps + parts):
+        pltpu.make_async_remote_copy(
+            src_ref=send.at[d - 1, pl.ds(a, b - a)], dst_ref=recv[n],
+            send_sem=z_send, recv_sem=z_recv.at[n],
+            device_id=z_peer(d), device_id_type=MESH,
+        ).start()
+
+    def wanted(d, ty, tx, pieces):
+        spot = unpack[d, (ty * nz + z) * nx + tx]
+        block = None
+        for ref, a, b in pieces:
+            one = ref[jnp.clip(spot - 1 - a, 0, b - a - 1)]
+            block = one if block is None else jnp.where(spot > a, one, block)
+        return jnp.where(spot > 0, block, jnp.zeros_like(block))
+
+    def own(ty, tx):
+        spot = unpack[0, (ty * nz + z) * nx + tx]
+        block = norm[pack[0, z * plane + jnp.maximum(spot, 1) - 1]]
+        return jnp.where(spot > 0, block, jnp.zeros_like(block))
+
+    def slot_from(d):
+        return (y * nz + lax.rem(z + nz - d, nz)) * nx + x
+
+    def p_copy(d, j, ty, tx):
+        return pltpu.make_async_remote_copy(
+            src_ref=stage.at[d, j], dst_ref=out.at[slot_from(d)],
+            send_sem=p_send, recv_sem=p_recv,
+            device_id=(ty, z, tx, g), device_id_type=MESH,
+        )
+
+    def deliver(d, block_for):
+        def target(j):
+            return lax.rem(y + lax.div(j, nx), ny), lax.rem(x + lax.rem(j, nx), nx)
+
+        @pl.loop(1, plane)
+        def _(j):
+            stage[d, j] = block_for(*target(j))
+
+        @pl.loop(1, plane)
+        def _(j):
+            p_copy(d, j, *target(j)).start()
+
+        out[slot_from(d)] = block_for(y, x)
+
+    deliver(0, own)
+    for n, (d, a, b) in enumerate(steps):
+        pltpu.make_async_copy(recv[n], recv[n], z_recv.at[n]).wait()
+        pieces = [(recv[n], a, b)]
+        deliver(d, lambda ty, tx: wanted(d, ty, tx, pieces))
+
+    pieces = []
+    for h in range(ny):
+        if h < len(parts):
+            n = len(steps) + h
+            pltpu.make_async_copy(recv[n], recv[n], z_recv.at[n]).wait()
+            pieces.append((recv[n], *parts[h][1:]))
+
+        def target(j):
+            ty = lax.rem(y + j, ny)
+            return ty, lax.rem(h + ny - ty, nx)
+
+        @pl.loop(0, nx)
+        def _(j):
+            stage[far, h * nx + j] = wanted(far, *target(j), pieces)
+
+        @pl.loop(0, nx)
+        def _(j):
+            ty, tx = target(j)
+
+            @pl.when((ty - y) * nx + tx - x != 0)
+            def _():
+                p_copy(far, h * nx + j, ty, tx).start()
+
+    out[slot_from(far)] = wanted(far, y, x, pieces)
+
+    pltpu.make_async_copy(send, send, z_send).wait()
+    landed = out.at[pl.ds(0, nz * (plane - 1))]
+    pltpu.make_async_copy(landed, landed, p_send).wait()
+    pltpu.make_async_copy(landed, landed, p_recv).wait()
 
 
 def body(features, session, owner_map):
     rows_dev, width = features.shape
     blocks = owner_map.shape[1]
     block_rows = rows_dev // blocks
-    row_count = lax.axis_size(ROW)
     sizes = tuple(lax.axis_size(name) for name in ROW_GRP)
-    slot_cap = max(1, 2 * blocks // row_count)
-    slots = row_count * slot_cap
+    ny, nz, nx, ng = sizes
+    plane = ny * nx
+    slot_cap = max(1, 2 * blocks // (plane * nz))
+    slots = plane * nz * slot_cap
     tiles = rows_dev // TILE
     reach = (MOST - 2) // rows_dev + 1
-    outgoing = pl.pallas_call(
+    norm, unpack, pack, most = pl.pallas_call(
         lambda *refs: prelude_kernel(sizes, reach, block_rows, slot_cap, *refs),
-        out_shape=jax.ShapeDtypeStruct((slots, block_rows, width), jnp.bfloat16),
+        out_shape=(
+            jax.ShapeDtypeStruct((blocks, block_rows, width), jnp.bfloat16),
+            jax.ShapeDtypeStruct((nz, slots), jnp.int32),
+            jax.ShapeDtypeStruct((1, slots), jnp.int32),
+            jax.ShapeDtypeStruct((1, TILE), jnp.int32),
+        ),
         in_specs=[pl.BlockSpec(memory_space=pltpu.HBM)] * 3,
-        out_specs=pl.BlockSpec(memory_space=pltpu.VMEM),
+        out_specs=[pl.BlockSpec(memory_space=pltpu.VMEM)] * 4,
         scratch_shapes=[
             pltpu.VMEM(owner_map.shape, jnp.int32),
             pltpu.VMEM((tiles, TILE), jnp.int32),
             pltpu.VMEM((rows_dev, width), jnp.float32),
             pltpu.VMEM((rows_dev, width), jnp.float32),
             pltpu.VMEM((rows_dev, TILE), jnp.float32),
-            pltpu.VMEM((blocks, block_rows, width), jnp.bfloat16),
             pltpu.VMEM((tiles, TILE), jnp.int32),
             pltpu.VMEM((tiles, TILE), jnp.int32),
-            pltpu.VMEM((1, slots), jnp.int32),
-            pltpu.SMEM((1, slots), jnp.int32),
             pltpu.VMEM((4, TILE), jnp.float32),
             pltpu.VMEM((reach, 4, TILE), jnp.float32),
+            pltpu.VMEM((1, slots), jnp.int32),
+            pltpu.VMEM((nz * ng - 1, 1, slots), jnp.int32),
+            pltpu.VMEM((1, slots), jnp.int32),
+            pltpu.VMEM((plane - 1, 1, slots), jnp.int32),
             pltpu.SemaphoreType.DMA((3,)),
-            pltpu.SemaphoreType.DMA,
-            pltpu.SemaphoreType.DMA,
-            pltpu.SemaphoreType.DMA,
-        ],
+        ]
+        + [pltpu.SemaphoreType.DMA] * 6,
         compiler_params=pltpu.CompilerParams(
             collective_id=0, has_side_effects=True, vmem_limit_bytes=24 << 20
         ),
         name="prelude",
     )(owner_map, session.reshape(tiles, TILE), features)
-    return lax.all_to_all(outgoing, ROW, split_axis=0, concat_axis=0, tiled=True)
+
+    def exchange(room, number):
+        block = (block_rows, width)
+        return lambda pack, unpack, norm: pl.pallas_call(
+            lambda *refs: exchange_kernel(sizes, room, *refs),
+            out_shape=jax.ShapeDtypeStruct((slots, *block), jnp.bfloat16),
+            in_specs=[
+                pl.BlockSpec(memory_space=pltpu.SMEM),
+                pl.BlockSpec(memory_space=pltpu.SMEM),
+                pl.BlockSpec(memory_space=pltpu.VMEM),
+            ],
+            out_specs=pl.BlockSpec(memory_space=pltpu.VMEM),
+            scratch_shapes=[
+                pltpu.VMEM((nz - 1, room, *block), jnp.bfloat16),
+                pltpu.VMEM((nz, plane, *block), jnp.bfloat16),
+                pltpu.SemaphoreType.DMA,
+                pltpu.SemaphoreType.DMA((nz + ny,)),
+                pltpu.SemaphoreType.DMA,
+                pltpu.SemaphoreType.DMA,
+            ]
+            + [
+                pltpu.VMEM((b - a, *block), jnp.bfloat16)
+                for group in arrivals(sizes, room)
+                for _, a, b in group
+            ],
+            compiler_params=pltpu.CompilerParams(
+                collective_id=number, has_side_effects=True, vmem_limit_bytes=24 << 20
+            ),
+            name=f"exchange_{room}",
+        )(pack, unpack, norm)
+
+    rooms = ROOMS
+    choice = sum((most[0, 0] > room).astype(jnp.int32) for room in rooms[:-1])
+    return lax.switch(
+        choice, [exchange(room, 1 + n) for n, room in enumerate(rooms)], pack, unpack, norm
+    )
 
 
 def solution(mesh):

time: 134 us -> 124 us (0.925)
  blocking collectives: 109 us -> 0 us
  Pallas kernels: 18.9 us -> 114 us
  local copies, waits for them, and re-layouts: 5.57 us -> 8.35 us
    all_to_all x1 -> x0, blocking collectives: 109 us -> none  [body(): lax.all_to_all(outgoing, ROW, split_axis=0, concat_axis=0, tiled=True)]
    pallas_call x0 -> x1, Pallas kernels: none -> 91.9 us  [exchange(): pl.pallas_call(lambda *refs: exchange_kernel(sizes, room, *refs), out_sha...]
    pallas_call x1, Pallas kernels: 18.9 us -> 22.4 us  [body(): pl.pallas_call(lambda *refs: prelude_kernel(sizes, reach, block_rows, slo...]
    unnamed x7, local copies, waits for them, and re-layouts: 5.57 us -> 8.35 us
where the time goes in v3:
time: 124 us; the launch traced here: 123 us
  Pallas kernels  114 us (92%)
  local copies, waits for them, and re-layouts  8.35 us (7%)
    pallas_call x1, Pallas kernels, exchange(): pl.pallas_call(lambda *refs: exchange_kernel(sizes, room, *refs), out_sha...  91.9 us
    pallas_call x1, Pallas kernels, body(): pl.pallas_call(lambda *refs: prelude_kernel(sizes, reach, block_rows, slo...  22.4 us
    unnamed x7, local copies, waits for them, and re-layouts  8.35 us

profile of v3, /device:TPU:32, one launch (start us, length us, event | category | flops | bytes accessed | tf_op | source)
XLA Modules:
  0.0 122.9 jit_solution(15564547786372612399)
XLA Ops:
  0.0 0.0 copy-start
  0.0 2.2 %copy-done = f32[4096,256]{1,0:T(8,128)S(1)} copy-done((f32[4096,256]{1,0:T(8,128)S(1)}, f32[4096,256]{1,0:T(8,128)}, u32[]{:S(2)}) %copy-start) | copy-done | bytes 4194328
  2.2 0.0 copy-start.1
  2.2 0.7 copy-done.1
  2.9 0.0 copy-start.2
  2.9 0.7 copy-done.2
  3.6 22.4 %prelude.1 = (bf16[64,64,256]{2,1,0:T(8,128)(2,1)S(1)}, s32[8,128]{1,0:T(8,128)S(1)}, s32[1,128]{1,0:T(1,128)S(1)}, s32[1,128]{1,0:T(1,128)S(1)}) custom-call(s32[1,64]{1,0:T(1,128)S(1)} %copy-done.2, s32[32,128]{1,0:T(8,128)S(1)} %bitcast.3, f32[4096,256]{1,0:T(8,128)S(1)} %copy-done), custom_call_target="tpu_custom_call" | custom-call | tf_op jit(solution)/shard_map/prelude/pallas_call | solution.py:396
  26.1 92.0 %conditional.1 = (bf16[128,64,256]{2,1,0:T(8,128)(2,1)}) conditional(s32[]{:T(128)} %bitcast.1, (s32[1,128]{1,0:T(1,128)S(1)}, s32[8,128]{1,0:T(8,128)S(1)}, bf16[64,64,256]{2,1,0:T(8,128)(2,1)S(1)}) %tuple.20, (s32[1,128]{1,0:T(1,128)S(1)}, s32[8,128]{1,0:T(8,128)S(1)}, ...), branch_computations={%region_0.0_spmd, %region_1.0_spmd, %region_2.0_spmd, %region_3.0_... | conditional | bytes 8 | solution.py:461
  26.1 91.9 %exchange_13.1 = bf16[128,64,256]{2,1,0:T(8,128)(2,1)} custom-call(s32[1,128]{1,0:T(1,128)S(1)} %get-tuple-element.44.refs_0_, s32[8,128]{1,0:T(8,128)S(1)} %get-tuple-element.45.refs_1_, bf16[64,64,256]{2,1,0:T(8,128)(2,1)S(1)} %get-tuple-element.46.refs_2_), custom_call_target="tpu_custom_call" | custom-call | tf_op jit(solution)/shard_map/cond/branch_1_fun/exchange_13/pallas_call | solution.py:431
  118.1 4.8 %copy.15 = bf16[128,64,256]{2,1,0:T(8,128)(2,1)} copy(bf16[128,64,256]{2,1,0:T(8,128)(2,1)} %get-tuple-element.64) | data formatting | bytes 8388608
Async XLA Ops:
  0.0 2.2 %copy-start = (f32[4096,256]{1,0:T(8,128)S(1)}, f32[4096,256]{1,0:T(8,128)}, u32[]{:S(2)}) copy-start(f32[4096,256]{1,0:T(8,128)} %refs_2_.1) | copy-start | bytes 12582916
  2.2 0.7 copy-start.1
  2.9 0.7 copy-start.2

commit v4 on v3

--- a/solution.py
+++ b/solution.py
@@ -380,6 +380,33 @@
     landed = out.at[pl.ds(0, nz * (plane - 1))]
     pltpu.make_async_copy(landed, landed, p_send).wait()
     pltpu.make_async_copy(landed, landed, p_recv).wait()
+
+
+def to_hbm_kernel(src, out, sem):
+    parts = sem.shape[0]
+    size = src.shape[0] // parts
+    copies = [
+        pltpu.make_async_copy(
+            src.at[pl.ds(n * size, size)], out.at[pl.ds(n * size, size)], sem.at[n]
+        )
+        for n in range(parts)
+    ]
+    for copy in copies:
+        copy.start()
+    for copy in copies:
+        copy.wait()
+
+
+def to_hbm(array):
+    return pl.pallas_call(
+        to_hbm_kernel,
+        out_shape=pltpu.HBM(array.shape, array.dtype),
+        in_specs=[pl.BlockSpec(memory_space=pltpu.VMEM)],
+        out_specs=pl.BlockSpec(memory_space=pltpu.HBM),
+        scratch_shapes=[pltpu.SemaphoreType.DMA((4,))],
+        compiler_params=pltpu.CompilerParams(vmem_limit_bytes=1 << 20),
+        name="to_hbm",
+    )(array)
 
 
 def body(features, session, owner_map):
@@ -424,13 +451,18 @@
             collective_id=0, has_side_effects=True, vmem_limit_bytes=24 << 20
         ),
         name="prelude",
-    )(owner_map, session.reshape(tiles, TILE), features)
+    )(
+        *(
+            pltpu.with_memory_space_constraint(arg, pltpu.HBM)
+            for arg in (owner_map, session.reshape(tiles, TILE), features)
+        )
+    )
 
     def exchange(room, number):
         block = (block_rows, width)
-        return lambda pack, unpack, norm: pl.pallas_call(
+        return lambda pack, unpack, norm: to_hbm(pl.pallas_call(
             lambda *refs: exchange_kernel(sizes, room, *refs),
-            out_shape=jax.ShapeDtypeStruct((slots, *block), jnp.bfloat16),
+            out_shape=pltpu.VMEM((slots, *block), jnp.bfloat16),
             in_specs=[
                 pl.BlockSpec(memory_space=pltpu.SMEM),
                 pl.BlockSpec(memory_space=pltpu.SMEM),
@@ -454,7 +486,7 @@
                 collective_id=number, has_side_effects=True, vmem_limit_bytes=24 << 20
             ),
             name=f"exchange_{room}",
-        )(pack, unpack, norm)
+        )(pack, unpack, norm))
 
     rooms = ROOMS
     choice = sum((most[0, 0] > room).astype(jnp.int32) for room in rooms[:-1])

time: 124 us -> 115 us (0.927)
  local copies, waits for them, and re-layouts: 8.35 us -> 0 us
    unnamed x7 -> x0, local copies, waits for them, and re-layouts: 8.35 us -> none
    pallas_call x0 -> x1, Pallas kernels: none -> 2.04 us  [to_hbm(): pl.pallas_call(to_hbm_kernel, out_shape=pltpu.HBM(array.shape, array.dtyp...]
    pallas_call x1, Pallas kernels: 91.9 us -> 90 us  [exchange(): pl.pallas_call(lambda *refs: exchange_kernel(sizes, room, *refs), out_sha...]
where the time goes in v4:
time: 115 us; the launch traced here: 114 us
  Pallas kernels  114 us (99%)
    pallas_call x1, Pallas kernels, exchange(): pl.pallas_call(lambda *refs: exchange_kernel(sizes, room, *refs), out_sha...  90 us
    pallas_call x1, Pallas kernels, body(): pl.pallas_call(lambda *refs: prelude_kernel(sizes, reach, block_rows, slo...  21.9 us

profile of v4, /device:TPU:32, one launch (start us, length us, event | category | flops | bytes accessed | tf_op | source)
XLA Modules:
  0.0 114.1 jit_solution(3480162863833304955)
XLA Ops:
  0.0 21.9 %prelude.1 = (bf16[64,64,256]{2,1,0:T(8,128)(2,1)S(1)}, s32[8,128]{1,0:T(8,128)S(1)}, s32[1,128]{1,0:T(1,128)S(1)}, s32[1,128]{1,0:T(1,128)S(1)}) custom-call(s32[1,64]{1,0:T(1,128)} %refs_0_.1, s32[32,128]{1,0:T(8,128)} %bitcast.7, f32[4096,256]{1,0:T(8,128)} %refs_2_.1), custom_call_target="tpu_custom_call" | custom-call | tf_op jit(solution)/shard_map/prelude/pallas_call | solution.py:423
  22.0 92.1 %conditional.1 = (bf16[128,64,256]{2,1,0:T(8,128)(2,1)}) conditional(s32[]{:T(128)} %bitcast.1, (s32[1,128]{1,0:T(1,128)S(1)}, s32[8,128]{1,0:T(8,128)S(1)}, bf16[64,64,256]{2,1,0:T(8,128)(2,1)S(1)}) %tuple.20, (s32[1,128]{1,0:T(1,128)S(1)}, s32[8,128]{1,0:T(8,128)S(1)}, ...), branch_computations={%region_0.0_spmd, %region_1.0_spmd, %region_2.0_spmd, %region_3.0_... | conditional | bytes 8 | solution.py:493
  22.1 90.0 %exchange_13.1.src = bf16[128,64,256]{2,1,0:T(8,128)(2,1)S(1)} custom-call(s32[1,128]{1,0:T(1,128)S(1)} %get-tuple-element.44.refs_0_, s32[8,128]{1,0:T(8,128)S(1)} %get-tuple-element.45.refs_1_, bf16[64,64,256]{2,1,0:T(8,128)(2,1)S(1)} %get-tuple-element.46.refs_2_), custom_call_target="tpu_custom_call" | custom-call | tf_op jit(solution)/shard_map/cond/branch_1_fun/exchange_13/pallas_call | solution.py:463
  112.1 2.0 %to_hbm.6 = bf16[128,64,256]{2,1,0:T(8,128)(2,1)} custom-call(bf16[128,64,256]{2,1,0:T(8,128)(2,1)S(1)} %exchange_13.1.src), custom_call_target="tpu_custom_call" | custom-call | tf_op jit(solution)/shard_map/cond/branch_1_fun/to_hbm/pallas_call | solution.py:401
